TPU v7x, 16 devices: a whole 2x2x2 slice. The times are simulated.
16 devices in a mesh: dp: 4 (over z, y), ep: 4 (over x, core).
Axes of the slice: x: 2, y: 2, z: 2, core: 2. Of those that a mesh axis runs over, the one named last changes fastest.
Arguments:
- dispatched: bfloat16 [16, 8, 1024, 2048], P('dp', 'ep'), parts along dimension 0
- w_gate: bfloat16 [8, 2048, 5632], P('ep')
- w_up: bfloat16 [8, 2048, 5632], P('ep')
- w_down: bfloat16 [8, 5632, 2048], P('ep')
- fill_count: int32 [16, 8], P('dp', 'ep'), parts along dimension 0
- slot_index: int32 [32768, 2], P(('dp', 'ep')), parts along dimension 0
- expert_id: int32 [32768, 2], P(('dp', 'ep')), parts along dimension 0
- gate_weight: float32 [32768, 2], P(('dp', 'ep')), parts along dimension 0
Outputs:
- output: bfloat16 [32768, 2048], P(('dp', 'ep')), parts along dimension 0
There are 4 independent parts. A program takes and returns all parts, laid end to end along the dimension named above; an argument that names none is the same for every part.
All inputs are finite; a program needn't handle non-finite values.
Results may differ from a plain program's by a relative error of at most 0.00134.
Values are sent between devices in bfloat16 or wider.
A program may use at most 1 GiB of HBM per device.

v0:
```python
import jax
import jax.numpy as jnp
from jax import lax
from jax.sharding import PartitionSpec as P


def expert_rows(dispatched, w_gate, w_up, w_down, fill_count):
    capacity = dispatched.shape[2]
    pre_gate = jnp.einsum("secd,edf->escf", dispatched, w_gate, preferred_element_type=jnp.float32)
    pre_up = jnp.einsum("secd,edf->escf", dispatched, w_up, preferred_element_type=jnp.float32)
    hidden = (jax.nn.silu(pre_gate) * pre_up).astype(jnp.bfloat16)
    result = jnp.einsum("escf,efd->escd", hidden, w_down, preferred_element_type=jnp.float32).astype(jnp.bfloat16)
    live_mask = jnp.arange(capacity)[None, None, :] < fill_count.T[:, :, None]
    return jnp.where(live_mask[..., None], result, 0)


def solution(mesh):
    def local_step(dispatched, w_gate, w_up, w_down, fill_count, slot_index, expert_id, gate_weight):
        result = expert_rows(dispatched, w_gate, w_up, w_down, fill_count)
        returned = lax.all_to_all(result, "ep", 1, 0, tiled=True)
        flat_rows = returned.reshape(-1, returned.shape[-1])
        row_index = expert_id * dispatched.shape[2] + jnp.maximum(slot_index, 0)
        picked = jnp.take(flat_rows, row_index, axis=0)
        weight = jnp.where(slot_index >= 0, gate_weight, 0.0)
        combined = jnp.sum(weight[:, :, None] * picked.astype(jnp.float32), axis=1)
        return combined.astype(jnp.bfloat16)
    token_spec = P(("dp", "ep"))
    in_specs = (P("dp", "ep"), P("ep"), P("ep"), P("ep"), P("dp", "ep"), token_spec, token_spec, token_spec)
    return jax.shard_map(local_step, mesh=mesh, in_specs=in_specs, out_specs=token_spec, check_vma=False)
```

profile of v0, /device:TPU:0, one launch (start us, length us, event | category | flops | bytes accessed | tf_op | source)
XLA Modules:
  0.0 1261.7 jit_solution(10768213268506371815)
XLA Ops:
  0.0 1.4 iota_compare_fusion
  1.4 203.2 %fusion.3 = f32[2,4,1024,5632]{3,2,1,0:T(8,128)} fusion(bf16[2,2048,5632]{2,1,0:T(8,128)(2,1)} %param.10, bf16[4,2,1024,2048]{3,2,1,0:T(8,128)(2,1)} %param.8), kind=kOutput, calls=%fused_computation.5 | convolution fusion | flops 188978561024 | bytes 264241152 | tf_op jit(solution)/shard_map/secd,edf->escf/dot_general | solution.py:10
  204.6 0.0 copy-start.3
  204.6 230.8 %multiply_convert_fusion.clone.6 = bf16[2,4,1024,5632]{3,2,1,0:T(8,128)(2,1)} fusion(f32[2,4,1024,5632]{3,2,1,0:T(8,128)} %fusion.3, bf16[2,2048,5632]{2,1,0:T(8,128)(2,1)} %param.9, bf16[4,2,1024,2048]{3,2,1,0:T(8,128)(2,1)} %param.8), kind=kOutput, calls=%fused_computation.1.clone.clone.clone.clone.clone.1 | convolution fusion | flops 189255385088 | bytes 356515840 | tf_op jit(solution)/shard_map/secd,edf->escf/dot_general | solution.py:9
  435.4 0.0 copy-done.3
  435.4 202.3 %convert_select_fusion = bf16[2,4,1024,2048]{3,2,1,0:T(8,128)(2,1)} fusion(pred[2,4,1024]{2,1,0:T(4,128)(4,1)S(1)} %copy-done.3, bf16[2,5632,2048]{2,1,0:T(8,128)(2,1)} %param.11, bf16[2,4,1024,5632]{3,2,1,0:T(8,128)(2,1)} %multiply_convert_fusion.clone.6), kind=kOutput, calls=%fused_computation.9 | convolution fusion | flops 189012115456 | bytes 171974656 | tf_op jit(solution)/shard_map/escf,efd->escd/dot_general | solution.py:12
  637.7 23.0 %copy.21 = bf16[2,4,1024,2048]{3,2,0,1:T(8,128)(2,1)} copy(bf16[2,4,1024,2048]{3,2,1,0:T(8,128)(2,1)} %convert_select_fusion) | data formatting | bytes 67108864 | tf_op jit(solution)/shard_map/jit(_where)/select_n | solution.py:14
  660.7 0.0 copy-start
  660.7 0.0 copy-start.1
  660.7 0.0 copy-start.2
  660.7 10.1 all-to-all-start
  670.8 0.0 copy-done
  670.8 0.0 copy-done.1
  670.9 0.4 copy.22
  671.2 0.5 reshape.18
  671.7 0.5 copy.18
  672.2 0.0 copy-done.2
  672.2 0.4 copy.17
  672.6 361.6 %all-to-all-done = bf16[2,4,1024,2048]{3,2,0,1:T(8,128)(2,1)} async-done(((bf16[2,4,1024,2048]{3,2,0,1:T(8,128)(2,1)}), bf16[2,4,1024,2048]{3,2,0,1:T(8,128)(2,1)}, u32[]{:S(2)}, u32[]{:S(2)}) %all-to-all-start) | async-done | bytes 33554464 | tf_op jit(solution)/shard_map/all_to_all | solution.py:20
  1034.2 125.1 %gather_fusion = bf16[4096,2048]{1,0:T(8,128)(2,1)} fusion(bf16[8192,2048]{1,0:T(8,128)(2,1)} %bitcast.9, s32[4096]{0:T(1024)S(1)} %broadcast_clamp_fusion), kind=kCustom, calls=%fused_computation | custom fusion | bytes 33570816 | tf_op jit(solution)/shard_map/jit(_take)/gather | solution.py:23
  1159.3 27.0 %reshape.17 = bf16[2048,2,2048]{2,1,0:T(2,128)(2,1)} reshape(bf16[4096,2048]{1,0:T(8,128)(2,1)} %gather_fusion) | data formatting | bytes 33554432 | tf_op jit(solution)/shard_map/jit(_take)/gather | solution.py:23
  1186.3 75.3 %multiply_reduce_fusion = bf16[2048,2048]{1,0:T(8,128)(2,1)} fusion(bf16[2048,2,2048]{2,1,0:T(2,128)(2,1)} %reshape.17, pred[2048,2]{1,0:T(8,128)(4,1)S(1)} %copy.18, f32[2048,2]{1,0:T(8,128)S(1)} %copy.17), kind=kLoop, calls=%fused_computation.8 | loop fusion | flops 29360128 | bytes 25186304 | tf_op jit(solution)/shard_map/reduce_sum | solution.py:25
  (3 shorter events, 0.1 us)
Async XLA Ops:
  204.6 230.8 %copy-start.3 = (pred[2,4,1024]{2,1,0:T(4,128)(4,1)S(1)}, pred[2,4,1024]{2,1,0:T(4,128)(4,1)}, u32[]{:S(2)}) copy-start(pred[2,4,1024]{2,1,0:T(4,128)(4,1)} %iota_compare_fusion) | copy-start | bytes 24580
  660.7 10.1 copy-start
  660.7 10.1 copy-start.1
  660.7 11.5 copy-start.2
  660.7 373.5 %all-to-all-start = ((bf16[2,4,1024,2048]{3,2,0,1:T(8,128)(2,1)}), bf16[2,4,1024,2048]{3,2,0,1:T(8,128)(2,1)}, u32[]{:S(2)}, u32[]{:S(2)}) async-start(bf16[2,4,1024,2048]{3,2,0,1:T(8,128)(2,1)} %copy.21), calls=%async_computation | async-start | bytes 67108864 | tf_op jit(solution)/shard_map/all_to_all | solution.py:20
where the time goes:
time: 1270 us; the launch traced here: 1260 us
  matrix products  636 us (50%)
  waiting for transfers between devices  362 us (29%)
  local copies, waits for them, and re-layouts  177 us (14%)
  other arithmetic  76.7 us (6%)
    all_to_all x1, waiting for transfers between devices, local_step(): returned = lax.all_to_all(result, 'ep', 1, 0, tiled=True)  362 us
    dot_general x1, matrix products, expert_rows(): jnp.einsum('secd,edf->escf', dispatched, w_gate, preferred_element_type=j...  231 us
    dot_general x1, matrix products, expert_rows(): jnp.einsum('secd,edf->escf', dispatched, w_up, preferred_element_type=jnp...  203 us
    dot_general x1, matrix products, expert_rows(): jnp.einsum('escf,efd->escd', hidden, w_down, preferred_element_type=jnp.f...  202 us
    gather x2, local copies, waits for them, and re-layouts, local_step(): picked = jnp.take(flat_rows, row_index, axis=0)  152 us
    reduce_sum x1, other arithmetic, local_step(): combined = jnp.sum(weight[:, :, None] * picked.astype(jnp.float32), axis=1)  75.3 us
  transfers between devices with their start and end apart: 1, of which 1 were waited for; matrix products, arithmetic and copies ran while one was open for 0% of the time, Pallas kernels for 0%

commit v1 on v0

v1 whole, which is shorter than its diff:
```python
import functools

import jax
import jax.numpy as jnp
from jax import lax
from jax.experimental import pallas as pl
from jax.experimental.pallas import tpu as pltpu
from jax.sharding import PartitionSpec as P


BIG, SMALL = 512, 256
CHUNK = 256
TOKENS = 512
VMEM_LIMIT = 58 * 1024 * 1024


def ffn_kernel(table, x_ref, gate_ref, up_ref, down_ref, y_ref, total):
    p, f = pl.program_id(0), pl.program_id(1)
    rows_filled = table[2, p]

    def tile(start, size):
        rows = pl.ds(pl.multiple_of(start, SMALL), size)
        x = x_ref[0, 0, rows, :]
        a = jnp.dot(x, gate_ref[0], preferred_element_type=jnp.float32)
        b = jnp.dot(x, up_ref[0], preferred_element_type=jnp.float32)
        h = (jax.nn.silu(a) * b).astype(jnp.bfloat16)
        y = jnp.dot(h, down_ref[0], preferred_element_type=jnp.float32)
        total[rows, :] = jnp.where(f == 0, 0.0, total[rows, :]) + y

    units = (rows_filled + SMALL - 1) >> 8
    pairs = units >> 1

    def pair(i, carry):
        tile(i * BIG, BIG)
        return carry

    lax.fori_loop(0, pairs, pair, 0)

    @pl.when((units & 1) == 1)
    def _():
        tile(pairs * BIG, SMALL)

    @pl.when(f == pl.num_programs(1) - 1)
    def _():
        def store(i, carry):
            rows = pl.ds(pl.multiple_of(i * SMALL, SMALL), SMALL)
            slot = i * SMALL + lax.broadcasted_iota(jnp.int32, (SMALL, 1), 0)
            y_ref[0, 0, rows, :] = jnp.where(slot < rows_filled, total[rows, :], 0.0).astype(jnp.bfloat16)
            return carry

        lax.fori_loop(0, units, store, 0)


def ffn(table, out_sources, x, w_gate, w_up, w_down, width=512):
    _, experts, capacity, hidden = x.shape
    width_all = w_gate.shape[2]
    last = width_all // width - 1

    def slice_of(p, f, t):
        return jnp.where(t[4, p] == 1, f, last)

    weight = pl.BlockSpec((1, hidden, width), lambda p, f, t: (t[1, p], 0, slice_of(p, f, t)))
    block = (1, 1, capacity, hidden)
    return pl.pallas_call(
        ffn_kernel,
        out_shape=jax.ShapeDtypeStruct((out_sources, experts, capacity, hidden), jnp.bfloat16),
        grid_spec=pltpu.PrefetchScalarGridSpec(
            num_scalar_prefetch=1,
            grid=(table.shape[1], last + 1),
            in_specs=[
                pl.BlockSpec(block, lambda p, f, t: (t[0, p], t[1, p], 0, 0)),
                weight,
                weight,
                pl.BlockSpec((1, width, hidden), lambda p, f, t: (t[1, p], slice_of(p, f, t), 0)),
            ],
            out_specs=pl.BlockSpec(block, lambda p, f, t: (t[3, p], t[1, p], 0, 0)),
            scratch_shapes=[pltpu.VMEM((capacity, hidden), jnp.float32)],
        ),
        compiler_params=pltpu.CompilerParams(
            dimension_semantics=("arbitrary", "arbitrary"), vmem_limit_bytes=VMEM_LIMIT
        ),
        cost_estimate=pl.CostEstimate(
            flops=6 * 1536 * out_sources * hidden * width_all,
            bytes_accessed=12 * out_sources * hidden * width_all,
            transcendentals=0,
        ),
    )(table, x, w_gate, w_up, w_down)


def combine_kernel(final, info, meta_ref, own_ref, part_ref, *refs):
    if final:
        helped_ref, z0_ref, z1_ref, out_ref, total = refs
    else:
        out_ref, total = refs
    q, t = pl.program_id(0), pl.program_id(1)
    tokens = pl.ds(pl.multiple_of(t * TOKENS, TOKENS), TOKENS)
    lane = lax.broadcasted_iota(jnp.int32, (TOKENS, meta_ref.shape[1]), 1)
    meta = meta_ref[...]
    slot = jnp.sum(jnp.where(lane == q, meta, 0.0), axis=1, keepdims=True)
    scale = jnp.sum(jnp.where(lane == q + 4, meta, 0.0), axis=1, keepdims=True)

    @pl.when((q == 0) & (info[7] == 1))
    def _():
        total[tokens, :] = jnp.zeros((TOKENS, total.shape[1]), jnp.float32)

    def add_from(ref):
        def add(k, carry):
            rows = pl.ds(pl.multiple_of(k * CHUNK, CHUNK), CHUNK)
            ids = (k * CHUNK + lax.broadcasted_iota(jnp.int32, (TOKENS, CHUNK), 1)).astype(jnp.float32)
            select = jnp.where(slot == ids, 1.0, 0.0).astype(jnp.bfloat16)
            picked = jnp.dot(select, ref[0, 0, rows, :], preferred_element_type=jnp.float32)
            total[tokens, :] += scale * picked
            return carry

        lax.fori_loop(0, (info[q] + CHUNK - 1) >> 8, add, 0)

    @pl.when(q < 2)
    def _():
        add_from(own_ref)

    if final:
        @pl.when((q >= 2) & (info[6] == 0))
        def _():
            add_from(part_ref)

        @pl.when((q >= 2) & (info[6] == 1))
        def _():
            add_from(helped_ref)
    else:
        @pl.when(q >= 2)
        def _():
            add_from(part_ref)

    @pl.when((q == 3) & (info[7] == 1))
    def _():
        if final:
            back = jnp.sum(jnp.where(lane == 8, meta, 0.0), axis=1, keepdims=True)

            def finish(z_ref):
                z = jnp.where(back > 0.0, z_ref[...].astype(jnp.float32), 0.0)
                out_ref[...] = (total[tokens, :] + back * z).astype(jnp.bfloat16)

            @pl.when(info[5] == 0)
            def _():
                finish(z0_ref)

            @pl.when(info[5] == 1)
            def _():
                finish(z1_ref)
        else:
            out_ref[...] = total[tokens, :].astype(jnp.bfloat16)


def combine(final, info, meta, own, part, *more):
    capacity, hidden = own.shape[2:]
    count, lanes = meta.shape
    block = (1, 1, capacity, hidden)
    in_specs = [
        pl.BlockSpec((TOKENS, lanes), lambda q, t, i: (t * i[7], 0)),
        pl.BlockSpec(block, lambda q, t, i: (i[4], jnp.minimum(q, 1) * i[7], 0, 0)),
        pl.BlockSpec(block, lambda q, t, i: (0, jnp.maximum(q - 2, 0) * i[7], 0, 0)),
    ]
    if final:
        in_specs += [
            pl.BlockSpec(block, lambda q, t, i: (0, jnp.maximum(q - 2, 0) * i[6], 0, 0)),
            pl.BlockSpec((TOKENS, hidden), lambda q, t, i: (jnp.where((q == 3) & (i[5] == 0), t, 0), 0)),
            pl.BlockSpec((TOKENS, hidden), lambda q, t, i: (jnp.where((q == 3) & (i[5] == 1), t, 0), 0)),
        ]
    return pl.pallas_call(
        functools.partial(combine_kernel, final),
        out_shape=jax.ShapeDtypeStruct((count, hidden), jnp.bfloat16),
        grid_spec=pltpu.PrefetchScalarGridSpec(
            num_scalar_prefetch=1,
            grid=(4, count // TOKENS),
            in_specs=in_specs,
            out_specs=pl.BlockSpec((TOKENS, hidden), lambda q, t, i: (jnp.where(q == 3, t * i[7], 0), 0)),
            scratch_shapes=[pltpu.VMEM((count, hidden), jnp.float32)],
        ),
        compiler_params=pltpu.CompilerParams(
            dimension_semantics=("arbitrary", "arbitrary"), vmem_limit_bytes=VMEM_LIMIT
        ),
        cost_estimate=pl.CostEstimate(
            flops=2 * 2048 * count * hidden, bytes_accessed=32 * count * hidden, transcendentals=0
        ),
    )(info, meta, own, part, *more)


def routing_meta(experts, slot_index, expert_id, gate_weight, on_chip, raw_single):
    here = (expert_id[:, :, None] == experts) & (slot_index >= 0)[:, :, None]
    slot = jnp.sum(jnp.where(here, slot_index[:, :, None] + 1, 0), axis=1) - 1
    factor = jnp.sum(jnp.where(here, gate_weight[:, :, None], 0.0), axis=1)
    if raw_single:
        factor = jnp.where(on_chip[:, None] == 2, factor, 1.0)
    return jnp.concatenate([slot.astype(jnp.float32), factor], axis=1)


def solution(mesh):
    def local_step(dispatched, w_gate, w_up, w_down, fill_count, slot_index, expert_id, gate_weight):
        me = lax.axis_index("ep")
        core, chip = me & 1, me >> 1
        partner, across = me ^ 1, me ^ 2
        first = 2 * (1 - chip)
        swap_core = [(0, 1), (1, 0), (2, 3), (3, 2)]
        swap_chip = [(0, 2), (2, 0), (1, 3), (3, 1)]

        def permute(value, pairs):
            return lax.ppermute(value, "ep", pairs)

        fill_there = permute(fill_count, swap_core)
        load_here, load_there = jnp.sum(fill_count), jnp.sum(fill_there)
        i_help = load_here + jnp.sum(fill_there[me]) < load_there
        get_help = load_there + jnp.sum(fill_count[partner]) < load_here

        valid = slot_index >= 0
        on_far = jnp.sum((valid & ((expert_id >> 2) != chip)).astype(jnp.int32), axis=1)
        pair_order = jnp.array([0, 1, 2, 3], jnp.int32)

        def chip_experts(owner):
            return jnp.where(pair_order < 2, 2 * owner + pair_order, 2 * (owner ^ 1) + pair_order - 2)

        far_meta = routing_meta(chip_experts(across), slot_index, expert_id, gate_weight, on_far, True)
        near_meta = routing_meta(chip_experts(me), slot_index, expert_id, gate_weight, on_far, False)
        far_weight = jnp.sum(jnp.where(valid & ((expert_id >> 2) != chip), gate_weight, 0.0), axis=1)
        back = jnp.where(on_far == 2, 1.0, jnp.where(on_far == 1, far_weight, 0.0))
        near_meta = jnp.concatenate([near_meta, back[:, None]], axis=1)
        served_meta = permute(far_meta, swap_chip)

        def table(sources, targets, experts_fills, active):
            columns = []
            for source, target, fills, on in zip(sources, targets, experts_fills, active):
                for e in range(2):
                    columns.append(jnp.stack([source, jnp.int32(e), fills[e] * on, target, on]))
            return jnp.stack(columns, axis=1).astype(jnp.int32)

        def info(source, slot_of_own, helped, active):
            fills = jnp.concatenate([fill_count[source], fill_there[source]]) * active
            return jnp.concatenate([fills, jnp.stack([slot_of_own, core, helped, active])]).astype(jnp.int32)

        zero, one = jnp.int32(0), jnp.int32(1)
        gate_there = permute(w_gate, swap_core)
        rows_there = permute(lax.dynamic_slice_in_dim(dispatched, partner, 1, 0), swap_core)

        first_table = table([first], [zero], [fill_count[first]], [one])
        second_table = table([first + 1], [zero], [fill_count[first + 1]], [one])
        y_first = ffn(first_table, 1, dispatched, w_gate, w_up, w_down)
        y_first_part = permute(y_first, [(1, 0), (3, 2)])
        up_sent, down_sent, y_first = lax.optimization_barrier((w_up, w_down, y_first))
        up_there, down_there = permute(up_sent, swap_core), permute(down_sent, swap_core)
        served0 = combine(False, info(first, zero, zero, 1 - core), served_meta, y_first, y_first_part)
        z0 = permute(served0, [(0, 2), (2, 0)])
        second_table, served0 = lax.optimization_barrier((second_table, served0))
        y_second = ffn(second_table, 1, dispatched, w_gate, w_up, w_down)
        y_second_part = permute(y_second, [(0, 1), (2, 3)])
        served1 = combine(False, info(first + 1, zero, zero, core), served_meta, y_second, y_second_part)
        z1 = permute(served1, [(1, 3), (3, 1)])

        serve_partner = 1 - get_help.astype(jnp.int32)
        local_table = jnp.where(
            (serve_partner == 0) & (jnp.arange(4) >= 2),
            jnp.stack([me, one, zero, zero, zero])[:, None],
            table([me, partner], [zero, one], [fill_count[me], fill_count[partner]], [one, one]),
        ).astype(jnp.int32)
        local_table, served1 = lax.optimization_barrier((local_table, served1))
        y_local = ffn(local_table, 2, dispatched, w_gate, w_up, w_down)
        y_part = permute(y_local[1:2], swap_core)
        helps = i_help.astype(jnp.int32)
        help_table = table([zero], [zero], [fill_there[me]], [helps])
        help_table = jnp.where((helps == 0) & (jnp.arange(5) == 1)[:, None], 0, help_table)
        help_table, y_local = lax.optimization_barrier((help_table, y_local))
        y_help = ffn(help_table, 1, rows_there, gate_there, up_there, down_there)
        return combine(True, info(me, zero, helps, one), near_meta, y_local, y_part, y_help, z0, z1)

    token_spec = P(("dp", "ep"))
    in_specs = (P("dp", "ep"), P("ep"), P("ep"), P("ep"), P("dp", "ep"), token_spec, token_spec, token_spec)

    return jax.shard_map(local_step, mesh=mesh, in_specs=in_specs, out_specs=token_spec, check_vma=False)
```

time: 1270 us -> 693 us (0.55)
  the two profiles are of different devices: /device:TPU:0 before, /device:TPU:13 now
where the time goes in v1:
time: 693 us
  Pallas kernels  459 us (66%)
  starting transfers between devices  167 us (24%)
  local copies, waits for them, and re-layouts  29.8 us (4%)
  waiting for transfers between devices  22.1 us (3%)
  other arithmetic  9.41 us (1%)
    pallas_call x4, Pallas kernels, ffn(): pl.pallas_call(ffn_kernel, out_shape=jax.ShapeDtypeStruct((out_sources, e...  369 us
    ppermute x11, starting transfers between devices, permute(): return lax.ppermute(value, 'ep', pairs)  167 us
    pallas_call x3, Pallas kernels, combine(): pl.pallas_call(functools.partial(combine_kernel, final), out_shape=jax.Sh...  90.2 us
    ppermute x11, waiting for transfers between devices, permute(): return lax.ppermute(value, 'ep', pairs)  22.1 us
  transfers between devices with their start and end apart: 11, of which 3 were waited for; matrix products, arithmetic and copies ran while one was open for 5% of the time, Pallas kernels for 51%

profile of v1, /device:TPU:13, one launch (start us, length us, event | category | flops | bytes accessed | tf_op | source)
XLA Modules:
  0.0 692.6 jit_solution(2886738343050511234)
XLA Ops:
  0.7 1.3 reduce_sum.90
  2.0 2.2 fusion.12
  6.2 0.8 fusion.3
  13.2 62.3 %shard_map.91.own_ref = bf16[1,2,1024,2048]{3,2,1,0:T(8,128)(2,1)} custom-call(s32[5,2]{1,0:T(8,128)} %copy.58.table, bf16[4,2,1024,2048]{3,2,1,0:T(8,128)(2,1)} %x_ref.5, bf16[2,2048,5632]{2,1,0:T(8,128)(2,1)} %gate_ref.5, bf16[2,2048,5632]{2,1,0:T(8,128)(2,1)} %up_ref.5, bf16[2,5632,2048]{2,1,0:T(8,128)(2,1)} %down_ref.5), custom_call_target="tpu_custom_call" | custom-call | flops 106300440576 | bytes 138412032 | tf_op jit(solution)/shard_map/pallas_call | solution.py:64
  75.5 66.8 %collective-permute-start.2 = (bf16[1,2,1024,2048]{3,2,1,0:T(8,128)(2,1)}, bf16[1,2,1024,2048]{3,2,1,0:T(8,128)(2,1)}, u32[]{:S(2)}, u32[]{:S(2)}) collective-permute-start(bf16[1,2,1024,2048]{3,2,1,0:T(8,128)(2,1)} %shard_map.91.own_ref), channel_id=1, source_target_pairs={{1,0},{3,2},{5,4},{7,6},{9,8},{11,10},{13,12},{15,14}} | collective-permute-start | bytes 25165832 | tf_op jit(solution)/shard_map/ppermute | solution.py:207
  146.4 1.4 copy.61.meta_ref
  147.8 4.3 collective-permute-done.2.part_ref
  152.1 10.3 %shard_map.92 = bf16[2048,2048]{1,0:T(8,128)(2,1)} custom-call(s32[8]{0:T(128)} %concatenate.27.info, f32[2048,8]{1,0:T(8,128)} %copy.61.meta_ref, bf16[1,2,1024,2048]{3,2,1,0:T(8,128)(2,1)} %shard_map.91.own_ref, bf16[1,2,1024,2048]{3,2,1,0:T(8,128)(2,1)} %collective-permute-done.2.part_ref), custom_call_target="tpu_custom_call" | custom-call | flops 17179869184 | bytes 134217728 | tf_op jit(solution)/shard_map/pallas_call | solution.py:169
  163.1 62.2 %shard_map.93.own_ref = bf16[1,2,1024,2048]{3,2,1,0:T(8,128)(2,1)} custom-call(s32[5,2]{1,0:T(8,128)} %copy.60.table, bf16[4,2,1024,2048]{3,2,1,0:T(8,128)(2,1)} %x_ref.5, bf16[2,2048,5632]{2,1,0:T(8,128)(2,1)} %gate_ref.5, bf16[2,2048,5632]{2,1,0:T(8,128)(2,1)} %up_ref.5, bf16[2,5632,2048]{2,1,0:T(8,128)(2,1)} %down_ref.5), custom_call_target="tpu_custom_call" | custom-call | flops 106300440576 | bytes 138412032 | tf_op jit(solution)/shard_map/pallas_call | solution.py:64
  225.3 1.5 collective-permute-start.3
  226.8 8.3 %constant_dynamic-slice_fusion = bf16[1,2,1024,2048]{3,2,1,0:T(8,128)(2,1)} fusion(bf16[4,2,1024,2048]{3,2,1,0:T(8,128)(2,1)} %x_ref.5, s32[]{:T(128)S(6)} %select_n.94), kind=kLoop, calls=%fused_computation.20 | loop fusion | bytes 16777220 | tf_op jit(solution)/shard_map/dynamic_slice | solution.py:241
  235.1 91.5 %collective-permute-start.5 = (bf16[1,2,1024,2048]{3,2,1,0:T(8,128)(2,1)}, bf16[1,2,1024,2048]{3,2,1,0:T(8,128)(2,1)}, u32[]{:S(2)}, u32[]{:S(2)}) collective-permute-start(bf16[1,2,1024,2048]{3,2,1,0:T(8,128)(2,1)} %constant_dynamic-slice_fusion), channel_id=1, source_target_pairs={{0,1},{1,0},{2,3},{3,2},{4,5},{5,4},{6,7},{7,6},{8,9},{9,8},{10,11... | collective-permute-start | bytes 25165832 | tf_op jit(solution)/shard_map/ppermute | solution.py:207
  327.1 1.3 fusion.4
  328.6 0.7 stack.123
  329.4 0.7 stack.125
  330.4 1.4 copy.62.meta_ref
  336.3 17.4 %collective-permute-done.3.part_ref = bf16[1,2,1024,2048]{3,2,1,0:T(8,128)(2,1)} collective-permute-done((bf16[1,2,1024,2048]{3,2,1,0:T(8,128)(2,1)}, bf16[1,2,1024,2048]{3,2,1,0:T(8,128)(2,1)}, u32[]{:S(2)}, u32[]{:S(2)}) %collective-permute-start.3) | collective-permute-done | bytes 8388640 | tf_op jit(solution)/shard_map/ppermute | solution.py:207
  353.7 3.9 collective-permute-start.9
  357.7 36.6 %shard_map.94 = bf16[2048,2048]{1,0:T(8,128)(2,1)} custom-call(s32[8]{0:T(128)} %concatenate.24.info, f32[2048,8]{1,0:T(8,128)} %copy.61.meta_ref, bf16[1,2,1024,2048]{3,2,1,0:T(8,128)(2,1)} %shard_map.93.own_ref, bf16[1,2,1024,2048]{3,2,1,0:T(8,128)(2,1)} %collective-permute-done.3.part_ref), custom_call_target="tpu_custom_call" | custom-call | flops 17179869184 | bytes 134217728 | tf_op jit(solution)/shard_map/pallas_call | solution.py:169
  394.3 120.6 %shard_map.95.own_ref = bf16[2,2,1024,2048]{3,2,1,0:T(8,128)(2,1)} custom-call(s32[5,4]{1,0:T(8,128)} %add_select_fusion.table, bf16[4,2,1024,2048]{3,2,1,0:T(8,128)(2,1)} %x_ref.5, bf16[2,2048,5632]{2,1,0:T(8,128)(2,1)} %gate_ref.5, bf16[2,2048,5632]{2,1,0:T(8,128)(2,1)} %up_ref.5, bf16[2,5632,2048]{2,1,0:T(8,128)(2,1)} %down_ref.5), custom_call_target="tpu_custom_call" | custom-call | flops 212600881152 | bytes 276824064 | tf_op jit(solution)/shard_map/pallas_call | solution.py:64
  514.9 8.4 %slice.78 = bf16[1,2,1024,2048]{3,2,1,0:T(8,128)(2,1)} slice(bf16[2,2,1024,2048]{3,2,1,0:T(8,128)(2,1)} %shard_map.95.own_ref), slice={[1:2], [0:2], [0:1024], [0:2048]} | slice | bytes 16777216 | tf_op jit(solution)/shard_map/slice | solution.py:265
  523.3 2.1 collective-permute-start.10
  525.5 123.8 %shard_map.96.refs_0_ = bf16[1,2,1024,2048]{3,2,1,0:T(8,128)(2,1)} custom-call(s32[5,2]{1,0:T(8,128)} %broadcast_select_fusion.1.table, bf16[1,2,1024,2048]{3,2,1,0:T(8,128)(2,1)} %collective-permute-done.5.x_ref, bf16[2,2048,5632]{2,1,0:T(8,128)(2,1)} %collective-permute-done.6.gate_ref, bf16[2,2048,5632]{2,1,0:T(8,128)(2,1)} %collective-permute-done.7.up_ref, ...), custom_call_target="tpu_custom_call" | custom-call | flops 106300440576 | bytes 138412032 | tf_op jit(solution)/shard_map/pallas_call | solution.py:64
  649.3 43.3 %shard_map.97 = bf16[2048,2048]{1,0:T(8,128)(2,1)} custom-call(s32[8]{0:T(128)} %concatenate.21.info, f32[2048,9]{1,0:T(8,128)} %copy.62.meta_ref, bf16[2,2,1024,2048]{3,2,1,0:T(8,128)(2,1)} %shard_map.95.own_ref, bf16[1,2,1024,2048]{3,2,1,0:T(8,128)(2,1)} %collective-permute-done.4.part_ref, bf16[1,2,1024,2048]{3,2,1,0:T(8,128)(2,1)} %shard_map.96.refs_0_, ...), custom_call_target="tpu_custom_call" | custom-call | flops 17179869184 | bytes 134217728 | tf_op jit(solution)/shard_map/pallas_call | solution.py:169
  (79 shorter events, 14.4 us)
Async XLA Ops:
  0.0 6.2 collective-permute-start
  13.2 129.6 %copy-start = (s32[2048,2]{0,1:T(2,128)S(1)}, s32[2048,2]{0,1:T(2,128)}, u32[]{:S(2)}) copy-start(s32[2048,2]{0,1:T(2,128)} %param.15) | copy-start | bytes 49156
  13.2 129.7 %copy-start.2 = (s32[2048,2]{0,1:T(2,128)S(1)}, s32[2048,2]{0,1:T(2,128)}, u32[]{:S(2)}) copy-start(s32[2048,2]{0,1:T(2,128)} %param.14) | copy-start | bytes 49156
  13.2 129.7 %copy-start.1 = (f32[2048,2]{0,1:T(2,128)S(1)}, f32[2048,2]{0,1:T(2,128)}, u32[]{:S(2)}) copy-start(f32[2048,2]{0,1:T(2,128)} %param.16) | copy-start | bytes 49156
  75.5 76.6 %collective-permute-start.2 = (bf16[1,2,1024,2048]{3,2,1,0:T(8,128)(2,1)}, bf16[1,2,1024,2048]{3,2,1,0:T(8,128)(2,1)}, u32[]{:S(2)}, u32[]{:S(2)}) collective-permute-start(bf16[1,2,1024,2048]{3,2,1,0:T(8,128)(2,1)} %shard_map.91.own_ref), channel_id=1, source_target_pairs={{1,0},{3,2},{5,4},{7,6},{9,8},{11,10},{13,12},{15,14}} | collective-permute-start | bytes 25165832 | tf_op jit(solution)/shard_map/ppermute | solution.py:207
  142.3 383.2 %collective-permute-start.6 = (bf16[2,2048,5632]{2,1,0:T(8,128)(2,1)}, bf16[2,2048,5632]{2,1,0:T(8,128)(2,1)}, u32[]{:S(2)}, u32[]{:S(2)}) collective-permute-start(bf16[2,2048,5632]{2,1,0:T(8,128)(2,1)} %gate_ref.5), channel_id=1, source_target_pairs={{0,1},{1,0},{2,3},{3,2},{4,5},{5,4},{6,7},{7,6},{8,9},{9,8},{10,11... | collective-permute-start | bytes 138412032 | tf_op jit(solution)/shard_map/ppermute | solution.py:207
  142.3 383.2 %collective-permute-start.7 = (bf16[2,2048,5632]{2,1,0:T(8,128)(2,1)}, bf16[2,2048,5632]{2,1,0:T(8,128)(2,1)}, u32[]{:S(2)}, u32[]{:S(2)}) collective-permute-start(bf16[2,2048,5632]{2,1,0:T(8,128)(2,1)} %up_ref.5), channel_id=1, source_target_pairs={{0,1},{1,0},{2,3},{3,2},{4,5},{5,4},{6,7},{7,6},{8,9},{9,8},{10,11... | collective-permute-start | bytes 138412032 | tf_op jit(solution)/shard_map/ppermute | solution.py:207
  142.8 382.7 %collective-permute-start.8 = (bf16[2,5632,2048]{2,1,0:T(8,128)(2,1)}, bf16[2,5632,2048]{2,1,0:T(8,128)(2,1)}, u32[]{:S(2)}, u32[]{:S(2)}) collective-permute-start(bf16[2,5632,2048]{2,1,0:T(8,128)(2,1)} %down_ref.5), channel_id=1, source_target_pairs={{0,1},{1,0},{2,3},{3,2},{4,5},{5,4},{6,7},{7,6},{8,9},{9,8},{10,11... | collective-permute-start | bytes 138412032 | tf_op jit(solution)/shard_map/ppermute | solution.py:207
  143.3 3.2 collective-permute-start.1
  225.3 101.3 %copy-start.3 = (s32[1,2]{0,1:T(2,128)S(1)}, s32[1,2]{0,1:T(2,128)}, u32[]{:S(2)}) copy-start(s32[1,2]{0,1:T(2,128)} %get-tuple-element.43) | copy-start | bytes 28
  225.3 106.5 %copy-start.6 = (s32[2]{0:T(128)S(1)}, s32[2]{0:T(128)}, u32[]{:S(2)}) copy-start(s32[2]{0:T(128)} %get-tuple-element.46) | copy-start | bytes 28
  225.3 106.5 %copy-start.9 = (s32[2]{0:T(128)S(1)}, s32[2]{0:T(128)}, u32[]{:S(2)}) copy-start(s32[2]{0:T(128)} %get-tuple-element.24) | copy-start | bytes 28
  225.3 109.0 %copy-start.4 = (s32[5,2]{0,1:T(2,128)S(1)}, s32[5,2]{0,1:T(2,128)}, u32[]{:S(2)}) copy-start(s32[5,2]{0,1:T(2,128)} %get-tuple-element.63) | copy-start | bytes 124
  225.3 109.1 %copy-start.5 = (s32[2]{0:T(128)S(1)}, s32[2]{0:T(128)}, u32[]{:S(2)}) copy-start(s32[2]{0:T(128)} %get-tuple-element.44) | copy-start | bytes 28
  225.3 109.1 %copy-start.8 = (s32[2]{0:T(128)S(1)}, s32[2]{0:T(128)}, u32[]{:S(2)}) copy-start(s32[2]{0:T(128)} %get-tuple-element.50) | copy-start | bytes 28
  225.3 109.7 %copy-start.7 = (s32[5]{0:T(128)S(1)}, s32[5]{0:T(128)}, u32[]{:S(2)}) copy-start(s32[5]{0:T(128)} %get-tuple-element.59) | copy-start | bytes 64
  225.3 128.4 %collective-permute-start.3 = (bf16[1,2,1024,2048]{3,2,1,0:T(8,128)(2,1)}, bf16[1,2,1024,2048]{3,2,1,0:T(8,128)(2,1)}, u32[]{:S(2)}, u32[]{:S(2)}) collective-permute-start(bf16[1,2,1024,2048]{3,2,1,0:T(8,128)(2,1)} %shard_map.93.own_ref), channel_id=1, source_target_pairs={{0,1},{2,3},{4,5},{6,7},{8,9},{10,11},{12,13},{14,15}} | collective-permute-start | bytes 25165832 | tf_op jit(solution)/shard_map/ppermute | solution.py:207
  235.1 288.2 %collective-permute-start.5 = (bf16[1,2,1024,2048]{3,2,1,0:T(8,128)(2,1)}, bf16[1,2,1024,2048]{3,2,1,0:T(8,128)(2,1)}, u32[]{:S(2)}, u32[]{:S(2)}) collective-permute-start(bf16[1,2,1024,2048]{3,2,1,0:T(8,128)(2,1)} %constant_dynamic-slice_fusion), channel_id=1, source_target_pairs={{0,1},{1,0},{2,3},{3,2},{4,5},{5,4},{6,7},{7,6},{8,9},{9,8},{10,11... | collective-permute-start | bytes 25165832 | tf_op jit(solution)/shard_map/ppermute | solution.py:207
  353.7 295.6 %collective-permute-start.9 = (bf16[2048,2048]{1,0:T(8,128)(2,1)}, bf16[2048,2048]{1,0:T(8,128)(2,1)}, u32[]{:S(2)}, u32[]{:S(2)}) collective-permute-start(bf16[2048,2048]{1,0:T(8,128)(2,1)} %shard_map.92), channel_id=1, source_target_pairs={{0,2},{2,0},{4,6},{6,4},{8,10},{10,8},{12,14},{14,12}} | collective-permute-start | bytes 25165832 | tf_op jit(solution)/shard_map/ppermute | solution.py:207
  523.3 126.0 %collective-permute-start.10 = (bf16[2048,2048]{1,0:T(8,128)(2,1)}, bf16[2048,2048]{1,0:T(8,128)(2,1)}, u32[]{:S(2)}, u32[]{:S(2)}) collective-permute-start(bf16[2048,2048]{1,0:T(8,128)(2,1)} %shard_map.94), channel_id=1, source_target_pairs={{1,3},{3,1},{5,7},{7,5},{9,11},{11,9},{13,15},{15,13}} | collective-permute-start | bytes 25165832 | tf_op jit(solution)/shard_map/ppermute | solution.py:207
  525.5 123.9 %collective-permute-start.4 = (bf16[1,2,1024,2048]{3,2,1,0:T(8,128)(2,1)}, bf16[1,2,1024,2048]{3,2,1,0:T(8,128)(2,1)}, u32[]{:S(2)}, u32[]{:S(2)}) collective-permute-start(bf16[1,2,1024,2048]{3,2,1,0:T(8,128)(2,1)} %slice.78), channel_id=1, source_target_pairs={{0,1},{1,0},{2,3},{3,2},{4,5},{5,4},{6,7},{7,6},{8,9},{9,8},{10,11... | collective-permute-start | bytes 25165832 | tf_op jit(solution)/shard_map/ppermute | solution.py:207
